TPU v7x, 32 devices: a whole 2x2x4 slice. The times are simulated.
32 devices in a mesh: gy: 8 (over z, x), gx: 4 (over y, core).
Axes of the slice: x: 2, y: 2, z: 4, core: 2. Of those that a mesh axis runs over, the one named last changes fastest.
Arguments:
- tall_factor: bfloat16 [8192, 2048], P('gy', 'gx'), may hold values from -6 to 6
- wide_factor: bfloat16 [2048, 4096], P('gy', 'gx'), may hold values from -0.125 to 0.125
- target: float32 [8192, 4096], P('gy', 'gx'), may hold values from -6 to 6
Outputs:
- product_sum: float32 [8192, 4096], P('gy', 'gx')
All inputs are finite; a program needn't handle non-finite values.
Results may differ from a plain program's by a relative error of at most 0.0003.
Values may be sent and summed in bfloat16 or wider, within the bound.
A program may use at most 128 MiB of HBM per device.

v0:
```python
import jax
import jax.numpy as jnp
from jax import lax
from jax.sharding import PartitionSpec as P


def taken_in(section, axis, dim, lap, start):

    def gathered(part):
        return lax.all_gather(part, axis, axis=dim, tiled=True)

    return lap(start, jax.tree.map(gathered, section), jnp.int32(0))


def join_panel(carry, left_panel, right_panel):
    return carry + jnp.dot(left_panel, right_panel, preferred_element_type=jnp.float32)


def on_device(tall_factor, wide_factor, target):
    begin = jnp.zeros((tall_factor.shape[0], wide_factor.shape[1]), jnp.float32)
    left_line = lax.all_gather(tall_factor, "gx", axis=1, tiled=True)

    def take_rows(carry, piece, start):
        left_piece = lax.dynamic_slice_in_dim(left_line, start, piece.shape[0], axis=1)
        return join_panel(carry, left_piece, piece)

    total = taken_in(wide_factor, "gy", 0, take_rows, begin)
    product_sum = target - total
    row_power = lax.psum(jnp.sum(product_sum * product_sum, axis=1), "gx")
    product_sum = (
        product_sum
        * lax.rsqrt(row_power / (product_sum.shape[1] * lax.axis_size("gx")) + 1e-06)[:, None]
    )
    return product_sum


def solution(mesh):
    return jax.shard_map(
        on_device,
        mesh=mesh,
        in_specs=(P("gy", "gx"), P("gy", "gx"), P("gy", "gx")),
        out_specs=P("gy", "gx"),
        check_vma=False,
    )
```

profile of v0, /device:TPU:0, one launch (start us, length us, event | category | flops | bytes accessed | tf_op | source)
XLA Modules:
  0.0 155.2 jit_solution(12691582396637993418)
XLA Ops:
  6.5 0.0 all-gather.3.cloned.1.call-start
  6.5 0.7 all-gather.3.cloned.1.call-update
  7.3 0.0 all-gather.5.cloned.1.call-start
  7.3 0.7 all-gather.5.cloned.1.call-update
  8.0 5.3 %copy.4 = f32[1024,1024]{0,1:T(8,128)} copy(f32[1024,1024]{1,0:T(8,128)} %param.5) | data formatting | bytes 8388608 | tf_op args[2]
  13.4 32.8 %all-gather.3.cloned.1.call-done = bf16[1024,2048]{1,0:T(8,128)(2,1)} async-done(((bf16[1024,512]{1,0:T(8,128)(2,1)}), bf16[1024,2048]{1,0:T(8,128)(2,1)}) %all-gather.3.cloned.1.call-update) | async-done | bytes 4194320 | tf_op jit(solution)/shard_map/all_gather | solution.py:21
  46.1 74.9 %all-gather.5.cloned.1.call-done = bf16[2048,1024]{1,0:T(8,128)(2,1)} async-done(((bf16[256,1024]{1,0:T(8,128)(2,1)}), bf16[2048,1024]{1,0:T(8,128)(2,1)}) %all-gather.5.cloned.1.call-update) | async-done | bytes 4194320 | tf_op jit(solution)/shard_map/all_gather | solution.py:10
  121.0 11.3 %multiply_reduce_fusion = (f32[1024]{0:T(1024)S(1)}, f32[1024,1024]{0,1:T(8,128)}) fusion(f32[1024,1024]{0,1:T(8,128)} %copy.4, bf16[1024,2048]{1,0:T(8,128)(2,1)} %all-gather.3.cloned.1.call-done, bf16[2048,1024]{1,0:T(8,128)(2,1)} %all-gather.5.cloned.1.call-done), kind=kOutput, calls=%fused_computation | convolution fusion | flops 4298112000 | bytes 16781312 | tf_op jit(solution)/shard_map/dot_general | solution.py:16
  132.4 5.6 %psum.7 = f32[1024]{0:T(1024)S(1)} all-reduce(f32[1024]{0:T(1024)S(1)} %get-tuple-element.5), channel_id=1, replica_groups=mesh['gy'=8,'gx'=4] {'gx'}, use_global_device_ids=true, to_apply=%region_1.0 | all-reduce | flops 1024 | bytes 8192 | tf_op jit(solution)/shard_map/psum | solution.py:29
  138.0 5.0 %broadcast_multiply_fusion = f32[1024,1024]{0,1:T(8,128)} fusion(f32[1024,1024]{0,1:T(8,128)} %get-tuple-element.6, f32[1024]{0:T(1024)S(1)} %add_rsqrt_fusion), kind=kLoop, calls=%fused_computation.1 | loop fusion | flops 1048576 | bytes 8392704 | tf_op jit(solution)/shard_map/mul | solution.py:31
  143.0 5.3 %copy.5 = f32[1024,1024]{1,0:T(8,128)} copy(f32[1024,1024]{0,1:T(8,128)} %broadcast_multiply_fusion) | data formatting | bytes 8388608 | tf_op jit(solution)/shard_map/mul | solution.py:31
  (1 shorter events, 0.0 us)
Async XLA Ops:
  6.5 39.6 %all-gather.3.cloned.1.call-start = ((), (), s32[]{:S(2)}) async-start(), calls=%async_computation | async-start | bytes 5242880 | tf_op jit(solution)/shard_map/all_gather | solution.py:21
  7.3 113.8 %all-gather.5.cloned.1.call-start = ((), (), s32[]{:S(2)}) async-start(), calls=%async_computation.1 | async-start | bytes 4718592 | tf_op jit(solution)/shard_map/all_gather | solution.py:10
Sparse Core Ops, SparseCore 0:
  8.9 37.1 all-gather.2
  48.2 72.7 all-gather.4
where the time goes:
time: 155 us
  waiting for transfers between devices  109 us (70%)
  between operations  13.4 us (9%)
  matrix products  11.3 us (7%)
  local copies, waits for them, and re-layouts  10.7 us (7%)
  blocking collectives  5.63 us (4%)
  other arithmetic  4.99 us (3%)
    all_gather x1, waiting for transfers between devices, gathered(): return lax.all_gather(part, axis, axis=dim, tiled=True)  74.9 us
    all_gather x1, waiting for transfers between devices, on_device(): left_line = lax.all_gather(tall_factor, 'gx', axis=1, tiled=True)  32.8 us
    dot_general x1, matrix products, join_panel(): jnp.dot(left_panel, right_panel, preferred_element_type=jnp.float32)  11.3 us
    psum x1, blocking collectives, on_device(): row_power = lax.psum(jnp.sum(product_sum * product_sum, axis=1), 'gx')  5.63 us
    unnamed x1, local copies, waits for them, and re-layouts  5.35 us
    mul x1, local copies, waits for them, and re-layouts, on_device(): product_sum * lax.rsqrt(row_power / (product_sum.shape[1] * lax.axis_size...  5.34 us
    mul x1, other arithmetic, on_device(): product_sum * lax.rsqrt(row_power / (product_sum.shape[1] * lax.axis_size...  4.98 us
  transfers between devices with their start and end apart: 2, of which 2 were waited for; matrix products, arithmetic and copies ran while one was open for 3% of the time, Pallas kernels for 0%

commit v1 on v0

--- a/solution.py
+++ b/solution.py
@@ -18,7 +18,12 @@
 
 def on_device(tall_factor, wide_factor, target):
     begin = jnp.zeros((tall_factor.shape[0], wide_factor.shape[1]), jnp.float32)
-    left_line = lax.all_gather(tall_factor, "gx", axis=1, tiled=True)
+    ring = [tall_factor]
+    for hop in range(3):
+        ring.append(lax.ppermute(ring[-1], "gx", [(dev, (dev + 1) % 4) for dev in range(4)]))
+    left_line = jnp.roll(
+        jnp.concatenate(ring[::-1], axis=1), (lax.axis_index("gx") + 1) * ring[0].shape[1], axis=1
+    )
 
     def take_rows(carry, piece, start):
         left_piece = lax.dynamic_slice_in_dim(left_line, start, piece.shape[0], axis=1)

time: 155 us -> 119 us (0.77)
  waiting for transfers between devices: 109 us -> 61 us
  local copies, waits for them, and re-layouts: 10.7 us -> 22.2 us
    all_gather x1, waiting for transfers between devices: 74.9 us -> 22.5 us  [gathered(): return lax.all_gather(part, axis, axis=dim, tiled=True)]
    ppermute x0 -> x3, waiting for transfers between devices: none -> 37.8 us  [on_device(): lax.ppermute(ring[-1], 'gx', [(dev, (dev + 1) % 4) for dev in range(4)])]
    all_gather x1 -> x0, waiting for transfers between devices: 32.8 us -> none  [on_device(): left_line = lax.all_gather(tall_factor, 'gx', axis=1, tiled=True)]
    unnamed x1 -> x10, local copies, waits for them, and re-layouts: 5.35 us -> 15.8 us
  transfers between devices with their start and end apart: 2 -> 4, of which waited for: 2 -> 4; matrix products, arithmetic and copies ran while one was open for 3% -> 14% of each run, Pallas kernels for 0% -> 0%
where the time goes in v1:
time: 119 us
  waiting for transfers between devices  61 us (51%)
  local copies, waits for them, and re-layouts  22.2 us (19%)
  between operations  13.4 us (11%)
  matrix products  11.3 us (9%)
  blocking collectives  5.63 us (5%)
  other arithmetic  4.99 us (4%)
    ppermute x3, waiting for transfers between devices, on_device(): lax.ppermute(ring[-1], 'gx', [(dev, (dev + 1) % 4) for dev in range(4)])  37.8 us
    all_gather x1, waiting for transfers between devices, gathered(): return lax.all_gather(part, axis, axis=dim, tiled=True)  22.5 us
    unnamed x10, local copies, waits for them, and re-layouts  15.8 us
    dot_general x1, matrix products, join_panel(): jnp.dot(left_panel, right_panel, preferred_element_type=jnp.float32)  11.3 us
    psum x1, blocking collectives, on_device(): row_power = lax.psum(jnp.sum(product_sum * product_sum, axis=1), 'gx')  5.63 us
    mul x1, local copies, waits for them, and re-layouts, on_device(): product_sum * lax.rsqrt(row_power / (product_sum.shape[1] * lax.axis_size...  5.34 us
    mul x1, other arithmetic, on_device(): product_sum * lax.rsqrt(row_power / (product_sum.shape[1] * lax.axis_size...  4.98 us
  transfers between devices with their start and end apart: 4, of which 4 were waited for; matrix products, arithmetic and copies ran while one was open for 14% of the time, Pallas kernels for 0%

profile of v1, /device:TPU:0, one launch (start us, length us, event | category | flops | bytes accessed | tf_op | source)
XLA Modules:
  0.0 119.1 jit_solution(4471778392054491980)
XLA Ops:
  6.5 0.0 copy-start
  6.5 0.0 all-gather.2.cloned.1.call-start
  6.5 0.7 all-gather.2.cloned.1.call-update
  7.3 0.5 collective-permute-start
  7.8 14.6 %collective-permute-done = bf16[1024,512]{1,0:T(8,128)(2,1)S(1)} collective-permute-done((bf16[1024,512]{1,0:T(8,128)(2,1)}, bf16[1024,512]{1,0:T(8,128)(2,1)S(1)}, u32[]{:S(2)}, u32[]{:S(2)}) %collective-permute-start) | collective-permute-done | bytes 1048608 | tf_op jit(solution)/shard_map/ppermute | solution.py:23
  22.4 0.0 collective-permute-start.1
  22.5 14.2 %collective-permute-done.1 = bf16[1024,512]{1,0:T(8,128)(2,1)S(1)} collective-permute-done((bf16[1024,512]{1,0:T(8,128)(2,1)S(1)}, bf16[1024,512]{1,0:T(8,128)(2,1)S(1)}, u32[]{:S(2)}, u32[]{:S(2)}) %collective-permute-start.1) | collective-permute-done | bytes 1048608 | tf_op jit(solution)/shard_map/ppermute | solution.py:23
  36.7 0.0 collective-permute-start.2
  36.7 5.3 %copy.4 = f32[1024,1024]{0,1:T(8,128)} copy(f32[1024,1024]{1,0:T(8,128)} %param.5) | data formatting | bytes 8388608 | tf_op args[2]
  42.0 9.0 %collective-permute-done.2 = bf16[1024,512]{1,0:T(8,128)(2,1)} collective-permute-done((bf16[1024,512]{1,0:T(8,128)(2,1)S(1)}, bf16[1024,512]{1,0:T(8,128)(2,1)}, u32[]{:S(2)}, u32[]{:S(2)}) %collective-permute-start.2) | collective-permute-done | bytes 1048608 | tf_op jit(solution)/shard_map/ppermute | solution.py:23
  51.0 2.4 %constant_dynamic-update-slice_fusion.7 = bf16[1024,4096]{1,0:T(8,128)(2,1)} fusion(bf16[1024,512]{1,0:T(8,128)(2,1)} %collective-permute-done.2), kind=kLoop, calls=%fused_computation.12 | loop fusion | bytes 2097152
  53.4 1.1 constant_dynamic-update-slice_fusion.6
  54.5 1.2 constant_dynamic-update-slice_fusion.5
  55.6 0.0 copy-done
  55.6 1.1 constant_dynamic-update-slice_fusion.4
  56.8 2.3 %constant_dynamic-update-slice_fusion.3 = bf16[1024,4096]{1,0:T(8,128)(2,1)} fusion(bf16[1024,4096]{1,0:T(8,128)(2,1)} %constant_dynamic-update-slice_fusion.4, bf16[1024,512]{1,0:T(8,128)(2,1)} %collective-permute-done.2), kind=kLoop, calls=%fused_computation.8 | loop fusion | bytes 2097152
  59.1 1.2 constant_dynamic-update-slice_fusion.2
  60.3 1.1 constant_dynamic-update-slice_fusion.1
  61.4 1.1 constant_dynamic-update-slice_fusion
  62.5 22.5 %all-gather.2.cloned.1.call-done = bf16[2048,1024]{1,0:T(8,128)(2,1)} async-done(((bf16[256,1024]{1,0:T(8,128)(2,1)}), bf16[2048,1024]{1,0:T(8,128)(2,1)}) %all-gather.2.cloned.1.call-update) | async-done | bytes 4194320 | tf_op jit(solution)/shard_map/all_gather | solution.py:10
  85.0 11.3 %multiply_reduce_fusion = (f32[1024]{0:T(1024)S(1)}, f32[1024,1024]{0,1:T(8,128)}) fusion(f32[1024,1024]{0,1:T(8,128)} %copy.4, bf16[2048,1024]{1,0:T(8,128)(2,1)} %all-gather.2.cloned.1.call-done, bf16[1024,4096]{1,0:T(8,128)(2,1)} %constant_dynamic-update-slice_fusion, s32[]{:T(128)S(6)} %select_n.14), kind=kOutput, calls=%fused_computation | convolution fusion | flops 4298112000 | bytes 16781316 | tf_op jit(solution)/shard_map/dot_general | solution.py:16
  96.3 5.6 %psum.7 = f32[1024]{0:T(1024)S(1)} all-reduce(f32[1024]{0:T(1024)S(1)} %get-tuple-element.5), channel_id=1, replica_groups=mesh['gy'=8,'gx'=4] {'gx'}, use_global_device_ids=true, to_apply=%region_1.2 | all-reduce | flops 1024 | bytes 8192 | tf_op jit(solution)/shard_map/psum | solution.py:34
  102.0 5.0 %broadcast_multiply_fusion = f32[1024,1024]{0,1:T(8,128)} fusion(f32[1024,1024]{0,1:T(8,128)} %get-tuple-element.6, f32[1024]{0:T(1024)S(1)} %add_rsqrt_fusion), kind=kLoop, calls=%fused_computation.3 | loop fusion | flops 1048576 | bytes 8392704 | tf_op jit(solution)/shard_map/mul | solution.py:36
  107.0 5.3 %copy.5 = f32[1024,1024]{1,0:T(8,128)} copy(f32[1024,1024]{0,1:T(8,128)} %broadcast_multiply_fusion) | data formatting | bytes 8388608 | tf_op jit(solution)/shard_map/mul | solution.py:36
  (1 shorter events, 0.0 us)
Async XLA Ops:
  6.5 49.1 %copy-start = (bf16[1024,512]{1,0:T(8,128)(2,1)S(1)}, bf16[1024,512]{1,0:T(8,128)(2,1)}, u32[]{:S(2)}) copy-start(bf16[1024,512]{1,0:T(8,128)(2,1)} %param.3) | copy-start | bytes 3145732
  6.5 78.5 %all-gather.2.cloned.1.call-start = ((), (), s32[]{:S(2)}) async-start(), calls=%async_computation | async-start | bytes 4718592 | tf_op jit(solution)/shard_map/all_gather | solution.py:10
  7.3 15.2 %collective-permute-start = (bf16[1024,512]{1,0:T(8,128)(2,1)}, bf16[1024,512]{1,0:T(8,128)(2,1)S(1)}, u32[]{:S(2)}, u32[]{:S(2)}) collective-permute-start(bf16[1024,512]{1,0:T(8,128)(2,1)} %param.3), channel_id=1, source_target_pairs={{0,1},{1,2},{2,3},{3,0},{4,5},{5,6},{6,7},{7,4},{8,9},{9,10},{10,1... | collective-permute-start | bytes 3145736 | tf_op jit(solution)/shard_map/ppermute | solution.py:23
  22.4 14.2 %collective-permute-start.1 = (bf16[1024,512]{1,0:T(8,128)(2,1)S(1)}, bf16[1024,512]{1,0:T(8,128)(2,1)S(1)}, u32[]{:S(2)}, u32[]{:S(2)}) collective-permute-start(bf16[1024,512]{1,0:T(8,128)(2,1)S(1)} %collective-permute-done), channel_id=1, source_target_pairs={{0,1},{1,2},{2,3},{3,0},{4,5},{5,6},{6,7},{7,4},{8,9},{9,10},{10,1... | collective-permute-start | bytes 3145736 | tf_op jit(solution)/shard_map/ppermute | solution.py:23
  36.7 14.3 %collective-permute-start.2 = (bf16[1024,512]{1,0:T(8,128)(2,1)S(1)}, bf16[1024,512]{1,0:T(8,128)(2,1)}, u32[]{:S(2)}, u32[]{:S(2)}) collective-permute-start(bf16[1024,512]{1,0:T(8,128)(2,1)S(1)} %collective-permute-done.1), channel_id=1, source_target_pairs={{0,1},{1,2},{2,3},{3,0},{4,5},{5,6},{6,7},{7,4},{8,9},{9,10},{10,1... | collective-permute-start | bytes 3145736 | tf_op jit(solution)/shard_map/ppermute | solution.py:23
Sparse Core Ops, SparseCore 0:
  9.5 75.4 all-gather.1
